TPU v7x, 32 devices: a whole 2x2x4 slice. The times are simulated.
32 devices in a mesh: groups: 2 (over x), dp: 16 (over z, y, core).
Axes of the slice: x: 2, y: 2, z: 4, core: 2. Of those that a mesh axis runs over, the one named last changes fastest.
Arguments:
- batch_counts: int32 [32], P(('groups', 'dp')), parts along dimension 0, may hold values from 1 to 4, 32 in all
- attn_out: bfloat16 [128, 7168], P(('groups', 'dp')), parts along dimension 0, may hold values from -6 to 6
- residual_in: bfloat16 [128, 7168], P(('groups', 'dp')), parts along dimension 0, may hold values from -64 to 64
- norm_gain: float32 [7168], replicated, may hold values from 0.5 to 1.5
- w_gate_up: bfloat16 [2, 18432, 7168], P(None, 'dp'), may hold values from -0.0625 to 0.0625
- w_down: bfloat16 [18432, 7168], P(None, 'dp'), may hold values from -0.046875 to 0.046875
- next_gain: float32 [7168], replicated, may hold values from 0.5 to 1.5
Outputs:
- hidden_out: bfloat16 [128, 7168], P(('groups', 'dp')), parts along dimension 0
- normed_out: bfloat16 [128, 7168], P(('groups', 'dp')), parts along dimension 0
There are 2 independent parts, one for each index of `groups`. A program takes and returns all parts, laid end to end along the dimension named above; an argument that names none is the same for every part. Nothing has to cross between parts.
Inputs may be any that keep to these rules, and one draw needn't show every extreme that they name: Rank r's occupied rows are its first batch_counts[r] slots; the counts sum to exactly 32, and some rank holds 4.
All inputs are finite; a program needn't handle non-finite values. No bound on the sum of `batch_counts` on one device may be relied on, other than what follows from the above.
Results may differ from a plain program's by a relative error of at most 0.0045.
Values may be sent and summed in bfloat16 or wider, within the bound.
A program may use at most 128 MiB of HBM per device.

v0:
```python
import jax
import jax.numpy as jnp
from jax import lax
from jax.sharding import PartitionSpec as P

EPSILON = 1e-06


def normalize(values, weight_gain):
    mean_square = jnp.mean(values * values, axis=-1, keepdims=True)
    return values * lax.rsqrt(mean_square + EPSILON) * weight_gain


def mlp_hidden(picked_rows, w_gate_up):
    both_parts = jnp.einsum(
        "rd,gfd->grf", picked_rows, w_gate_up, preferred_element_type=jnp.float32
    )
    return (jax.nn.silu(both_parts[0]) * both_parts[1]).astype(jnp.bfloat16)


def on_device(batch_counts, attn_out, residual_in, norm_gain, w_gate_up, w_down, next_gain):
    slot_count = attn_out.shape[0]
    occupied = lax.broadcasted_iota(jnp.int32, (slot_count, 1), 0) < batch_counts[0]
    summed = residual_in.astype(jnp.float32) + attn_out.astype(jnp.float32)
    normed_in = normalize(summed, norm_gain).astype(jnp.bfloat16)
    hidden_rows = mlp_hidden(lax.all_gather(normed_in, "dp", axis=0, tiled=True), w_gate_up)
    down_cols = jnp.dot(
        lax.all_gather(hidden_rows, "dp", axis=1, tiled=True),
        w_down,
        preferred_element_type=jnp.float32,
    )
    mlp_out = lax.all_to_all(
        down_cols.astype(jnp.bfloat16), "dp", split_axis=0, concat_axis=1, tiled=True
    )
    updated = summed + mlp_out.astype(jnp.float32)
    hidden_out = jnp.where(occupied, updated, 0.0).astype(jnp.bfloat16)
    normed_out = jnp.where(occupied, normalize(updated, next_gain), 0.0).astype(jnp.bfloat16)
    return (hidden_out, normed_out)


def solution(mesh):
    placed = (
        P(("groups", "dp")),
        P(("groups", "dp"), None),
        P(("groups", "dp"), None),
        P(),
        P(None, "dp", None),
        P(None, "dp"),
        P(),
    )
    return jax.shard_map(
        on_device,
        mesh=mesh,
        in_specs=placed,
        out_specs=(P(("groups", "dp"), None), P(("groups", "dp"), None)),
        check_vma=False,
    )
```

profile of v0, /device:TPU:0, one launch (start us, length us, event | category | flops | bytes accessed | tf_op | source)
XLA Modules:
  0.0 121.2 jit_solution(10895494308429920050)
XLA Ops:
  7.2 0.0 all-gather.3.cloned.1.call-start
  7.2 1.0 multiply_reduce_fusion.1
  8.2 0.9 fusion.3
  9.2 25.9 %all-gather = bf16[16,4,7168]{2,1,0:T(4,128)(2,1)S(1)} all-gather(bf16[1,4,7168]{2,1,0:T(4,128)(2,1)S(1)} %fusion.3), channel_id=1, replica_groups=mesh['groups'=2,'dp'=16] {'dp'}, dimensions={0}, use_global_device_ids=true | all-gather | bytes 974848 | tf_op jit(solution)/shard_map/all_gather | solution.py:26
  35.1 0.2 reshape.35
  35.3 14.8 %convolution_bitcast_fusion = f32[2,64,1152]{2,1,0:T(8,128)S(1)} fusion(bf16[64,7168,1]{1,0,2:T(8,128)(2,1)S(1)} %reshape.35, bf16[2,1152,7168]{2,1,0:T(8,128)(2,1)} %param.11), kind=kOutput, calls=%fused_computation | convolution fusion | flops 2113929216 | bytes 34537472 | tf_op jit(solution)/shard_map/rd,gfd->grf/dot_general | solution.py:15
  50.1 0.0 copy-start
  50.1 0.0 copy-start.1
  50.1 0.0 copy-start.2
  50.1 0.7 fusion.1
  50.9 0.0 all-gather.3.cloned.1.call-update
  51.5 39.5 %all-gather.3.cloned.1.call-done = bf16[64,18432]{1,0:T(8,128)(2,1)} async-done(((bf16[64,1152]{1,0:T(8,128)(2,1)}), bf16[64,18432]{1,0:T(8,128)(2,1)}) %all-gather.3.cloned.1.call-update) | async-done | bytes 2359312 | tf_op jit(solution)/shard_map/all_gather | solution.py:28
  91.0 11.2 %convolution_convert_fusion = bf16[64,448]{1,0:T(8,128)(2,1)S(1)} fusion(bf16[64,18432]{1,0:T(8,128)(2,1)} %all-gather.3.cloned.1.call-done, bf16[18432,448]{0,1:T(8,128)(2,1)} %param.12), kind=kOutput, calls=%fused_computation.1 | convolution fusion | flops 1056993280 | bytes 18931712 | tf_op jit(solution)/shard_map/dot_general | solution.py:27
  102.2 0.6 all_to_all.10
  102.9 3.5 %all-to-all-start = ((bf16[16,4,448]{2,1,0:T(4,128)(2,1)}), bf16[16,4,448]{2,1,0:T(4,128)(2,1)S(1)}, u32[]{:S(2)}, u32[]{:S(2)}) async-start(bf16[16,4,448]{2,1,0:T(4,128)(2,1)} %all_to_all.10), calls=%async_computation | async-start | bytes 131072 | tf_op jit(solution)/shard_map/all_to_all | solution.py:32
  106.4 6.8 %all-to-all-done = bf16[16,4,448]{2,1,0:T(4,128)(2,1)S(1)} async-done(((bf16[16,4,448]{2,1,0:T(4,128)(2,1)}), bf16[16,4,448]{2,1,0:T(4,128)(2,1)S(1)}, u32[]{:S(2)}, u32[]{:S(2)}) %all-to-all-start) | async-done | bytes 57376 | tf_op jit(solution)/shard_map/all_to_all | solution.py:32
  113.3 0.1 reshape.32
  113.4 0.0 copy-done
  113.4 0.0 copy-done.1
  113.4 0.2 multiply_reduce_fusion
  113.6 0.0 copy-done.2
  113.6 0.8 select_convert_fusion
  (5 shorter events, 0.1 us)
Async XLA Ops:
  7.2 83.8 %all-gather.3.cloned.1.call-start = ((), (), s32[]{:S(2)}) async-start(), calls=%async_computation.1 | async-start | bytes 2506752 | tf_op jit(solution)/shard_map/all_gather | solution.py:28
  50.1 63.3 %copy-start = (bf16[4,7168]{1,0:T(4,128)(2,1)S(1)}, bf16[4,7168]{1,0:T(4,128)(2,1)}, u32[]{:S(2)}) copy-start(bf16[4,7168]{1,0:T(4,128)(2,1)} %param.8) | copy-start | bytes 172036
  50.1 63.3 %copy-start.1 = (bf16[4,7168]{1,0:T(4,128)(2,1)S(1)}, bf16[4,7168]{1,0:T(4,128)(2,1)}, u32[]{:S(2)}) copy-start(bf16[4,7168]{1,0:T(4,128)(2,1)} %param.9) | copy-start | bytes 172036
  50.1 63.5 %copy-start.2 = (f32[7168]{0:T(1024)S(1)}, f32[7168]{0:T(1024)}, u32[]{:S(2)}) copy-start(f32[7168]{0:T(1024)} %param.13) | copy-start | bytes 86020
  102.9 10.4 %all-to-all-start = ((bf16[16,4,448]{2,1,0:T(4,128)(2,1)}), bf16[16,4,448]{2,1,0:T(4,128)(2,1)S(1)}, u32[]{:S(2)}, u32[]{:S(2)}) async-start(bf16[16,4,448]{2,1,0:T(4,128)(2,1)} %all_to_all.10), calls=%async_computation | async-start | bytes 131072 | tf_op jit(solution)/shard_map/all_to_all | solution.py:32
Sparse Core Ops, SparseCore 0:
  51.0 39.9 all-gather.2
where the time goes:
time: 122 us; the launch traced here: 121 us
  waiting for transfers between devices  46.3 us (38%)
  matrix products  26 us (21%)
  blocking collectives  25.9 us (21%)
  between operations  14.8 us (12%)
  other arithmetic  3.69 us (3%)
  starting transfers between devices  3.53 us (3%)
    all_gather x1, waiting for transfers between devices, on_device(): lax.all_gather(hidden_rows, 'dp', axis=1, tiled=True)  39.5 us
    all_gather x1, blocking collectives, on_device(): lax.all_gather(normed_in, 'dp', axis=0, tiled=True)  25.9 us
    dot_general x1, matrix products, mlp_hidden(): jnp.einsum('rd,gfd->grf', picked_rows, w_gate_up, preferred_element_type=...  14.8 us
    dot_general x1, matrix products, on_device(): jnp.dot(lax.all_gather(hidden_rows, 'dp', axis=1, tiled=True), w_down, pr...  11.2 us
    all_to_all x1, waiting for transfers between devices, on_device(): lax.all_to_all(down_cols.astype(jnp.bfloat16), 'dp', split_axis=0, concat...  6.85 us
    all_to_all x1, starting transfers between devices, on_device(): lax.all_to_all(down_cols.astype(jnp.bfloat16), 'dp', split_axis=0, concat...  3.49 us
  transfers between devices with their start and end apart: 2, of which 2 were waited for; matrix products, arithmetic and copies ran while one was open for 0% of the time, Pallas kernels for 0%

commit v1 on v0

--- a/solution.py
+++ b/solution.py
@@ -1,6 +1,10 @@
+import functools
+
 import jax
 import jax.numpy as jnp
 from jax import lax
+from jax.experimental import pallas as pl
+from jax.experimental.pallas import tpu as pltpu
 from jax.sharding import PartitionSpec as P
 
 EPSILON = 1e-06
@@ -18,7 +22,7 @@
     return (jax.nn.silu(both_parts[0]) * both_parts[1]).astype(jnp.bfloat16)
 
 
-def on_device(batch_counts, attn_out, residual_in, norm_gain, w_gate_up, w_down, next_gain):
+def plain_layer(batch_counts, attn_out, residual_in, norm_gain, w_gate_up, w_down, next_gain):
     slot_count = attn_out.shape[0]
     occupied = lax.broadcasted_iota(jnp.int32, (slot_count, 1), 0) < batch_counts[0]
     summed = residual_in.astype(jnp.float32) + attn_out.astype(jnp.float32)
@@ -38,6 +42,344 @@
     return (hidden_out, normed_out)
 
 
+LANES = 128
+SUBLANES = 16
+CHUNKS = 3
+MESH = pl.DeviceIdType.MESH
+NT = (((1,), (1,)), ((), ()))
+
+
+def dot(a, b):
+    return jnp.dot(a, b, preferred_element_type=jnp.float32)
+
+
+class Gather:
+    def __init__(self, n, at, send_sem, recv_sem):
+        self.n, self.far_count = n, n // 4
+        self.me = lax.axis_index("dp")
+        self.core, self.near, self.far = self.me % 2, (self.me // 2) % 2, self.me // 4
+        self.sibling = self.index(0, self.near, 1 - self.core)
+        self.across = self.index(0, 1 - self.near, self.core)
+        self.at, self.send_sem, self.recv_sem = at, send_sem, recv_sem
+        self.sent = []
+
+    def index(self, back, near, core):
+        far = lax.rem(self.far - back + self.far_count, self.far_count)
+        return (far * 2 + near) * 2 + core
+
+    def copy(self, block, target, slot):
+        return pltpu.make_async_remote_copy(
+            src_ref=self.at(block),
+            dst_ref=self.at(block),
+            send_sem=self.send_sem(slot),
+            recv_sem=self.recv_sem(block),
+            device_id={"dp": target},
+            device_id_type=MESH,
+        )
+
+    def send(self, block, target):
+        copy = self.copy(block, target, len(self.sent))
+        copy.start()
+        self.sent.append(copy)
+
+    def await_block(self, block):
+        self.copy(block, self.sibling, 0).wait_recv()
+
+    def far_order(self):
+        steps = list(range(1, self.far_count))
+        return sorted(steps, key=lambda d: min(d, self.far_count - d))
+
+    def start(self):
+        for back in reversed(self.far_order()):
+            self.send(self.me, self.index(back, self.near, self.core))
+        self.send(self.me, self.across)
+        self.send(self.me, self.sibling)
+
+    def after_far(self):
+        for back in self.far_order():
+            block = self.index(back, self.near, self.core)
+            self.await_block(block)
+            self.send(block, self.across)
+            self.send(block, self.sibling)
+
+    def after_near(self):
+        for back in [0] + self.far_order():
+            block = self.index(back, 1 - self.near, self.core)
+            self.await_block(block)
+            self.send(block, self.sibling)
+
+    def after_core(self):
+        for near in (self.near, 1 - self.near):
+            for back in [0] + self.far_order():
+                self.await_block(self.index(back, near, 1 - self.core))
+
+    def drain(self):
+        for copy in self.sent:
+            copy.wait_send()
+
+
+def layer_kernel(
+    n, live,
+    counts_ref, attn_hbm, residual_hbm, gain_hbm, gate_up_hbm, down_hbm, next_gain_hbm,
+    hidden_ref, normed_ref,
+    attn, residual, gain, next_gain, gate_up, down,
+    summed_ref, packed_ref, rows_ref, picked_ref, act_ref, wide_ref, out_ref, back_ref, flat_ref,
+    small_sem, weight_sem, down_sem, row_send, row_recv, act_send, act_recv, out_send, out_recv,
+):
+    me = lax.axis_index("dp")
+    slots, width = attn.shape
+    pack = SUBLANES // slots
+    quarter = width // pack
+    piece = gate_up.shape[1] // CHUNKS
+
+    barrier = pltpu.get_barrier_semaphore()
+    for step in range(1, n):
+        pl.semaphore_signal(
+            barrier, inc=1, device_id={"dp": lax.rem(me + step, n)}, device_id_type=MESH
+        )
+    small = [
+        pltpu.make_async_copy(source, target, small_sem.at[k])
+        for k, (source, target) in enumerate(
+            [(attn_hbm, attn), (residual_hbm, residual), (gain_hbm, gain), (next_gain_hbm, next_gain)]
+        )
+    ]
+    for copy in small:
+        copy.start()
+    weight_copies = []
+    for c in range(CHUNKS):
+        for g in range(2):
+            span = pl.ds(c * piece, piece)
+            copy = pltpu.make_async_copy(
+                gate_up_hbm.at[g, span], gate_up.at[g, span], weight_sem.at[c * 2 + g]
+            )
+            copy.start()
+            weight_copies.append(copy)
+    down_copies = []
+    for c in range(4):
+        span = pl.ds(c * (n // 4), n // 4)
+        copy = pltpu.make_async_copy(down_hbm.at[span], down.at[span], down_sem.at[c])
+        copy.start()
+        down_copies.append(copy)
+    for copy in small:
+        copy.wait()
+
+    count = counts_ref[0]
+    summed = residual[...].astype(jnp.float32) + attn[...].astype(jnp.float32)
+    summed_ref[...] = summed
+    normed = normalize(summed, gain[...])
+    for q in range(pack):
+        packed_ref[q * slots:(q + 1) * slots, :quarter] = normed[:, q * quarter:(q + 1) * quarter]
+    packed_ref[:, quarter:] = jnp.full((SUBLANES, LANES), count, jnp.int32).astype(jnp.float32)
+    rows_ref[me] = packed_ref[...].astype(jnp.bfloat16)
+    wide_ref[...] = jnp.zeros_like(wide_ref)
+
+    pl.semaphore_wait(barrier, n - 1)
+    rows = Gather(
+        n, lambda b: rows_ref.at[b], lambda k: row_send.at[k], lambda b: row_recv.at[b]
+    )
+    rows.start()
+    rows.after_far()
+    rows.after_near()
+    rows.after_core()
+
+    total = n * SUBLANES
+    counts = rows_ref[:, :, quarter:].reshape(total, LANES)
+    at_row = lax.broadcasted_iota(jnp.int32, (total, total), 0)
+    at_col = lax.broadcasted_iota(jnp.int32, (total, total), 1)
+    one_before = (at_row % SUBLANES == 0) & (at_row // SUBLANES < at_col // SUBLANES)
+    one_before = one_before.astype(jnp.float32).astype(jnp.bfloat16)
+    mean_lane = jnp.full((live, LANES), 1.0 / LANES, jnp.bfloat16)
+    held = lax.dot_general(mean_lane, counts, NT, preferred_element_type=jnp.float32)
+    first = dot(held.astype(jnp.bfloat16), one_before)
+    token = lax.broadcasted_iota(jnp.int32, (live, total), 0).astype(jnp.float32)
+    place = lax.broadcasted_iota(jnp.int32, (live, total), 1)
+    slot = (place % slots).astype(jnp.float32)
+    chosen = (slot < held) & (first + slot == token)
+    all_rows = rows_ref[:, :, :quarter].reshape(total, quarter)
+    for q in range(pack):
+        pick = jnp.where(chosen & (place // slots % pack == q), 1.0, 0.0).astype(jnp.bfloat16)
+        picked_ref[:, q * quarter:(q + 1) * quarter] = dot(pick, all_rows).astype(jnp.bfloat16)
+
+    acts = [
+        Gather(
+            n,
+            lambda b, c=c: act_ref.at[b, c],
+            lambda k, c=c: act_send.at[c, k],
+            lambda b, c=c: act_recv.at[c, b],
+        )
+        for c in range(CHUNKS)
+    ]
+
+    def hidden(c):
+        span = slice(c * piece, (c + 1) * piece)
+        weight_copies[2 * c].wait()
+        gate = lax.dot_general(
+            picked_ref[...], gate_up[0, span, :], NT, preferred_element_type=jnp.float32
+        )
+        weight_copies[2 * c + 1].wait()
+        up = lax.dot_general(
+            picked_ref[...], gate_up[1, span, :], NT, preferred_element_type=jnp.float32
+        )
+        act_ref[me, c] = (gate / (1.0 + jnp.exp(-gate)) * up).astype(jnp.bfloat16)
+        acts[c].start()
+
+    def project(c, total_out):
+        def one(s, held_out):
+            return held_out + dot(act_ref[s, c], down[s, c * piece:(c + 1) * piece, :])
+
+        return lax.fori_loop(0, n, one, total_out)
+
+    hidden(0)
+    hidden(1)
+    acts[0].after_far()
+    hidden(2)
+    acts[0].after_near()
+    acts[1].after_far()
+    for copy in down_copies:
+        copy.wait()
+    acts[0].after_core()
+    projected = project(0, jnp.zeros((live, down.shape[2]), jnp.float32))
+    acts[1].after_near()
+    acts[2].after_far()
+    acts[1].after_core()
+    projected = project(1, projected)
+    acts[2].after_near()
+    acts[2].after_core()
+    projected = project(2, projected)
+
+    depth = down.shape[2]
+    wide_ref[:, :depth] = projected
+    wide = wide_ref[...]
+    half = depth % LANES
+    if half:
+        wide = jnp.where(me % 2 == 1, pltpu.roll(wide, half, 1), wide)
+    wide = wide.astype(jnp.bfloat16)
+    tall = jnp.concatenate([wide[:, q * LANES:(q + 1) * LANES] for q in range(pack)], axis=0)
+    before = (at_col % SUBLANES == 0) & (at_col // SUBLANES < at_row // SUBLANES)
+    start_of = dot(before.astype(jnp.float32).astype(jnp.bfloat16), counts)[:, :1]
+    back_place = lax.broadcasted_iota(jnp.int32, (total, pack * live), 0)
+    back_lane = lax.broadcasted_iota(jnp.int32, (total, pack * live), 1)
+    back_slot = (back_place % slots).astype(jnp.float32)
+    hit = (
+        (back_slot < counts[:, :1].astype(jnp.float32))
+        & (start_of + back_slot == (back_lane % live).astype(jnp.float32))
+        & (back_place // slots % pack == back_lane // live)
+    )
+    out_ref[...] = (
+        dot(jnp.where(hit, 1.0, 0.0).astype(jnp.bfloat16), tall)
+        .astype(jnp.bfloat16)
+        .reshape(n, SUBLANES, LANES)
+    )
+
+    def out_copy(source, target, k):
+        return pltpu.make_async_remote_copy(
+            src_ref=out_ref.at[target],
+            dst_ref=back_ref.at[source],
+            send_sem=out_send.at[k],
+            recv_sem=out_recv.at[source],
+            device_id={"dp": target},
+            device_id_type=MESH,
+        )
+
+    outs = [out_copy(me, lax.rem(me + step, n), step) for step in range(1, n)]
+    for copy in outs:
+        copy.start()
+    back_ref[me] = out_ref[me]
+    rows.drain()
+    for act in acts:
+        act.drain()
+    for step in range(1, n):
+        source = lax.rem(me + step, n)
+        out_copy(source, source, step).wait_recv()
+
+    flat_ref[...] = back_ref[...].reshape(total, LANES).astype(jnp.float32)
+    for s in range(n):
+        for q in range(pack):
+            tile = s * depth // LANES + q
+            if tile * LANES < width:
+                span = slice(tile * LANES, (tile + 1) * LANES)
+                row = s * SUBLANES + q * slots
+                summed_ref[:, span] = summed_ref[:, span] + flat_ref[row:row + slots, :]
+    updated = summed_ref[...]
+    occupied = lax.broadcasted_iota(jnp.int32, (slots, 1), 0) < count
+    hidden_ref[...] = jnp.where(occupied, updated, 0.0).astype(jnp.bfloat16)
+    normed_out = normalize(updated, next_gain[...])
+    normed_ref[...] = jnp.where(occupied, normed_out, 0.0).astype(jnp.bfloat16)
+    for copy in outs:
+        copy.wait_send()
+
+
+def fused_layer(n, batch_counts, attn_out, residual_in, norm_gain, w_gate_up, w_down, next_gain):
+    slots, width = attn_out.shape
+    hidden_units = w_gate_up.shape[1]
+    depth = w_down.shape[1]
+    live = n * slots // 2
+    pack = SUBLANES // slots
+    bf16, f32 = jnp.bfloat16, jnp.float32
+    sems = pltpu.SemaphoreType.DMA
+    anywhere = pl.BlockSpec(memory_space=pl.ANY)
+    in_vmem = pl.BlockSpec(memory_space=pltpu.VMEM)
+    return pl.pallas_call(
+        functools.partial(layer_kernel, n, live),
+        out_shape=[jax.ShapeDtypeStruct((slots, width), bf16)] * 2,
+        in_specs=[pl.BlockSpec(memory_space=pltpu.SMEM)] + [anywhere] * 6,
+        out_specs=[in_vmem, in_vmem],
+        scratch_shapes=[
+            pltpu.VMEM((slots, width), bf16),
+            pltpu.VMEM((slots, width), bf16),
+            pltpu.VMEM((1, width), f32),
+            pltpu.VMEM((1, width), f32),
+            pltpu.VMEM(w_gate_up.shape, bf16),
+            pltpu.VMEM((n, hidden_units, depth), bf16),
+            pltpu.VMEM((slots, width), f32),
+            pltpu.VMEM((SUBLANES, width // pack + LANES), f32),
+            pltpu.VMEM((n, SUBLANES, width // pack + LANES), bf16),
+            pltpu.VMEM((live, width), bf16),
+            pltpu.VMEM((n, CHUNKS, live, hidden_units // CHUNKS), bf16),
+            pltpu.VMEM((live, pack * LANES), f32),
+            pltpu.VMEM((n, SUBLANES, LANES), bf16),
+            pltpu.VMEM((n, SUBLANES, LANES), bf16),
+            pltpu.VMEM((n * SUBLANES, LANES), f32),
+            sems((4,)),
+            sems((2 * CHUNKS,)),
+            sems((4,)),
+            sems((n,)),
+            sems((n,)),
+            sems((CHUNKS, n)),
+            sems((CHUNKS, n)),
+            sems((n,)),
+            sems((n,)),
+        ],
+        compiler_params=pltpu.CompilerParams(
+            collective_id=0, has_side_effects=True, vmem_limit_bytes=65 * 1000 * 1000
+        ),
+    )(
+        batch_counts,
+        attn_out,
+        residual_in,
+        norm_gain.reshape(1, width),
+        w_gate_up,
+        w_down.reshape(n, hidden_units, depth),
+        next_gain.reshape(1, width),
+    )
+
+
+def on_device(n, *arrays):
+    slots, width = arrays[1].shape
+    hidden_units, depth = arrays[4].shape[1], arrays[5].shape[1]
+    pack = SUBLANES // slots
+    fused = (
+        n % 4 == 0
+        and SUBLANES % slots == 0
+        and width % (pack * LANES) == 0
+        and hidden_units % (CHUNKS * LANES) == 0
+        and n * slots // 2 * pack == LANES
+        and depth % (LANES // 2) == 0
+        and depth + depth % LANES <= pack * LANES
+    )
+    return tuple(fused_layer(n, *arrays)) if fused else plain_layer(*arrays)
+
+
 def solution(mesh):
     placed = (
         P(("groups", "dp")),
@@ -49,7 +391,7 @@
         P(),
     )
     return jax.shard_map(
-        on_device,
+        functools.partial(on_device, mesh.shape["dp"]),
         mesh=mesh,
         in_specs=placed,
         out_specs=(P(("groups", "dp"), None), P(("groups", "dp"), None)),

time: 122 us -> 87.8 us (0.72)
  Pallas kernels: 0 us -> 60.8 us
  waiting for transfers between devices: 46.3 us -> 0 us
  matrix products: 26 us -> 0 us
  blocking collectives: 25.9 us -> 0 us
  local copies, waits for them, and re-layouts: 1.04 us -> 25 us
  between operations: 14.8 us -> 1.28 us
  other arithmetic: 3.69 us -> 0 us
  starting transfers between devices: 3.53 us -> 0 us
    pallas_call x0 -> x1, Pallas kernels: none -> 60.8 us  [fused_layer(): pl.pallas_call(functools.partial(layer_kernel, n, live), out_shape=[jax.S...]
    all_gather x1 -> x0, waiting for transfers between devices: 39.5 us -> none  [on_device(): lax.all_gather(hidden_rows, 'dp', axis=1, tiled=True)]
    dot_general x2 -> x0, matrix products: 26 us -> none  [the longest x1 14.8 us: mlp_hidden(): jnp.einsum('rd,gfd->grf', picked_rows, w_gate_up, preferred_element_type=...]
    all_gather x1 -> x0, blocking collectives: 25.9 us -> none  [on_device(): lax.all_gather(normed_in, 'dp', axis=0, tiled=True)]
    unnamed x7 -> x3, local copies, waits for them, and re-layouts: 0.22 us -> 25 us
    all_to_all x1 -> x0, waiting for transfers between devices: 6.85 us -> none  [on_device(): lax.all_to_all(down_cols.astype(jnp.bfloat16), 'dp', split_axis=0, concat...]
    all_to_all x1 -> x0, starting transfers between devices: 3.49 us -> none  [on_device(): lax.all_to_all(down_cols.astype(jnp.bfloat16), 'dp', split_axis=0, concat...]
    convert_element_type x3 -> x0, other arithmetic: 1.52 us -> none  [the longest x1 0.76 us: on_device(): jnp.where(occupied, normalize(updated, next_gain), 0.0).astype(jnp.bfloat16)]
  transfers between devices with their start and end apart: 2 -> 0, of which waited for: 2 -> 0; matrix products, arithmetic and copies ran while one was open for 0% -> 0% of each run, Pallas kernels for 0% -> 0%
where the time goes in v1:
time: 87.8 us; the launch traced here: 87.1 us
  Pallas kernels  60.8 us (69%)
  local copies, waits for them, and re-layouts  25 us (28%)
  between operations  1.28 us (1%)
    pallas_call x1, Pallas kernels, fused_layer(): pl.pallas_call(functools.partial(layer_kernel, n, live), out_shape=[jax.S...  60.8 us
    unnamed x3, local copies, waits for them, and re-layouts  25 us

profile of v1, /device:TPU:0, one launch (start us, length us, event | category | flops | bytes accessed | tf_op | source)
XLA Modules:
  0.0 87.1 jit_solution(9723595330762203531)
XLA Ops:
  1.3 22.1 %copy.9 = bf16[18432,448]{1,0:T(8,128)(2,1)} copy(bf16[18432,448]{0,1:T(8,128)(2,1)} %param.12) | data formatting | bytes 33030144 | tf_op args[5]
  23.4 60.8 %shard_map.86 = (bf16[4,7168]{1,0:T(4,128)(2,1)}, bf16[4,7168]{1,0:T(4,128)(2,1)}) custom-call(s32[1]{0:T(128)S(6)} %copy.12.counts_ref, bf16[4,7168]{1,0:T(4,128)(2,1)} %attn_hbm.1, bf16[4,7168]{1,0:T(4,128)(2,1)} %residual_hbm.1, f32[1,7168]{1,0:T(1,128)} %bitcast.4, bf16[2,1152,7168]{2,1,0:T(8,128)(2,1)} %gate_up_hbm.1, bf16[16,1152,448]{2,1,0:T(8,128)(2,1)} %bitcast.3, ...), custom_call_target="tpu_custom_call" | custom-call | tf_op jit(solution)/shard_map/pallas_call | solution.py:322
  84.1 1.5 %copy.13 = bf16[4,7168]{1,0:T(4,128)(2,1)} copy(bf16[4,7168]{1,0:T(4,128)(2,1)} %get-tuple-element.4) | data formatting | bytes 114688
  85.6 1.5 %copy.14 = bf16[4,7168]{1,0:T(4,128)(2,1)} copy(bf16[4,7168]{1,0:T(4,128)(2,1)} %get-tuple-element.5) | data formatting | bytes 114688

commit v2 on v1

--- a/solution.py
+++ b/solution.py
@@ -45,12 +45,20 @@
 LANES = 128
 SUBLANES = 16
 CHUNKS = 3
+MXU_DEPTH = 256
 MESH = pl.DeviceIdType.MESH
 NT = (((1,), (1,)), ((), ()))
 
 
 def dot(a, b):
     return jnp.dot(a, b, preferred_element_type=jnp.float32)
+
+
+def chunk_bounds(units):
+    depths = units // MXU_DEPTH
+    sizes = [MXU_DEPTH * ((depths + CHUNKS - 1 - c) // CHUNKS) for c in range(CHUNKS)]
+    sizes[1] += units - sum(sizes)
+    return [(sum(sizes[:c]), sizes[c]) for c in range(CHUNKS)]
 
 
 class Gather:
@@ -58,13 +66,13 @@
         self.n, self.far_count = n, n // 4
         self.me = lax.axis_index("dp")
         self.core, self.near, self.far = self.me % 2, (self.me // 2) % 2, self.me // 4
-        self.sibling = self.index(0, self.near, 1 - self.core)
-        self.across = self.index(0, 1 - self.near, self.core)
+        self.sibling = self.index(self.far, self.near, 1 - self.core)
+        self.across = self.index(self.far, 1 - self.near, self.core)
         self.at, self.send_sem, self.recv_sem = at, send_sem, recv_sem
         self.sent = []
-
-    def index(self, back, near, core):
-        far = lax.rem(self.far - back + self.far_count, self.far_count)
+        self.lines = list(self.far_lines())
+
+    def index(self, far, near, core):
         return (far * 2 + near) * 2 + core
 
     def copy(self, block, target, slot):
@@ -85,33 +93,41 @@
     def await_block(self, block):
         self.copy(block, self.sibling, 0).wait_recv()
 
-    def far_order(self):
-        steps = list(range(1, self.far_count))
-        return sorted(steps, key=lambda d: min(d, self.far_count - d))
+    def far_lines(self):
+        count = self.far_count
+        ranked = [
+            sorted((p for p in range(count) if p != here), key=lambda p: abs(p - here))
+            for here in range(count)
+        ]
+        for k in range(count - 1):
+            far = ranked[0][k]
+            for here in range(1, count):
+                far = jnp.where(self.far == here, ranked[here][k], far)
+            yield far
 
     def start(self):
-        for back in reversed(self.far_order()):
-            self.send(self.me, self.index(back, self.near, self.core))
+        for far in reversed(self.lines):
+            self.send(self.me, self.index(far, self.near, self.core))
         self.send(self.me, self.across)
         self.send(self.me, self.sibling)
 
     def after_far(self):
-        for back in self.far_order():
-            block = self.index(back, self.near, self.core)
+        for far in self.lines:
+            block = self.index(far, self.near, self.core)
             self.await_block(block)
             self.send(block, self.across)
             self.send(block, self.sibling)
 
     def after_near(self):
-        for back in [0] + self.far_order():
-            block = self.index(back, 1 - self.near, self.core)
+        for far in [self.far] + self.lines:
+            block = self.index(far, 1 - self.near, self.core)
             self.await_block(block)
             self.send(block, self.sibling)
 
     def after_core(self):
         for near in (self.near, 1 - self.near):
-            for back in [0] + self.far_order():
-                self.await_block(self.index(back, near, 1 - self.core))
+            for far in [self.far] + self.lines:
+                self.await_block(self.index(far, near, 1 - self.core))
 
     def drain(self):
         for copy in self.sent:
@@ -120,17 +136,19 @@
 
 def layer_kernel(
     n, live,
-    counts_ref, attn_hbm, residual_hbm, gain_hbm, gate_up_hbm, down_hbm, next_gain_hbm,
-    hidden_ref, normed_ref,
-    attn, residual, gain, next_gain, gate_up, down,
-    summed_ref, packed_ref, rows_ref, picked_ref, act_ref, wide_ref, out_ref, back_ref, flat_ref,
+    counts_hbm, attn_hbm, residual_hbm, gain_hbm, gate_up_hbm, down_hbm,
+    updated_ref,
+    counts_ref, attn, residual, gain, gate_up, down,
+    summed_ref, packed_ref, rows_ref, picked_ref, act_refs, wide_ref, out_ref, back_ref, flat_ref,
     small_sem, weight_sem, down_sem, row_send, row_recv, act_send, act_recv, out_send, out_recv,
 ):
     me = lax.axis_index("dp")
     slots, width = attn.shape
     pack = SUBLANES // slots
     quarter = width // pack
-    piece = gate_up.shape[1] // CHUNKS
+    units = gate_up.shape[1]
+    pieces = chunk_bounds(units)
+    depth = down.shape[0]
 
     barrier = pltpu.get_barrier_semaphore()
     for step in range(1, n):
@@ -140,15 +158,17 @@
     small = [
         pltpu.make_async_copy(source, target, small_sem.at[k])
         for k, (source, target) in enumerate(
-            [(attn_hbm, attn), (residual_hbm, residual), (gain_hbm, gain), (next_gain_hbm, next_gain)]
+            [(attn_hbm, attn), (residual_hbm, residual), (gain_hbm, gain), (counts_hbm, counts_ref)]
         )
     ]
     for copy in small:
         copy.start()
+    for copy in small:
+        copy.wait()
     weight_copies = []
     for c in range(CHUNKS):
         for g in range(2):
-            span = pl.ds(c * piece, piece)
+            span = pl.ds(*pieces[c])
             copy = pltpu.make_async_copy(
                 gate_up_hbm.at[g, span], gate_up.at[g, span], weight_sem.at[c * 2 + g]
             )
@@ -156,12 +176,10 @@
             weight_copies.append(copy)
     down_copies = []
     for c in range(4):
-        span = pl.ds(c * (n // 4), n // 4)
+        span = pl.ds(c * (depth // 4), depth // 4)
         copy = pltpu.make_async_copy(down_hbm.at[span], down.at[span], down_sem.at[c])
         copy.start()
         down_copies.append(copy)
-    for copy in small:
-        copy.wait()
 
     count = counts_ref[0]
     summed = residual[...].astype(jnp.float32) + attn[...].astype(jnp.float32)
@@ -203,7 +221,7 @@
     acts = [
         Gather(
             n,
-            lambda b, c=c: act_ref.at[b, c],
+            lambda b, c=c: act_refs[c].at[b],
             lambda k, c=c: act_send.at[c, k],
             lambda b, c=c: act_recv.at[c, b],
         )
@@ -211,7 +229,8 @@
     ]
 
     def hidden(c):
-        span = slice(c * piece, (c + 1) * piece)
+        first_unit, size = pieces[c]
+        span = slice(first_unit, first_unit + size)
         weight_copies[2 * c].wait()
         gate = lax.dot_general(
             picked_ref[...], gate_up[0, span, :], NT, preferred_element_type=jnp.float32
@@ -220,14 +239,17 @@
         up = lax.dot_general(
             picked_ref[...], gate_up[1, span, :], NT, preferred_element_type=jnp.float32
         )
-        act_ref[me, c] = (gate / (1.0 + jnp.exp(-gate)) * up).astype(jnp.bfloat16)
+        act_refs[c][me] = (gate / (1.0 + jnp.exp(-gate)) * up).astype(jnp.bfloat16)
         acts[c].start()
 
     def project(c, total_out):
-        def one(s, held_out):
-            return held_out + dot(act_ref[s, c], down[s, c * piece:(c + 1) * piece, :])
-
-        return lax.fori_loop(0, n, one, total_out)
+        first_unit, size = pieces[c]
+        for s in range(n):
+            span = slice(s * units + first_unit, s * units + first_unit + size)
+            total_out += lax.dot_general(
+                down[:, span], act_refs[c][s], NT, preferred_element_type=jnp.float32
+            )
+        return total_out
 
     hidden(0)
     hidden(1)
@@ -238,7 +260,7 @@
     for copy in down_copies:
         copy.wait()
     acts[0].after_core()
-    projected = project(0, jnp.zeros((live, down.shape[2]), jnp.float32))
+    projected = project(0, jnp.zeros((depth, live), jnp.float32))
     acts[1].after_near()
     acts[2].after_far()
     acts[1].after_core()
@@ -247,8 +269,7 @@
     acts[2].after_core()
     projected = project(2, projected)
 
-    depth = down.shape[2]
-    wide_ref[:, :depth] = projected
+    wide_ref[:, :depth] = projected.T
     wide = wide_ref[...]
     half = depth % LANES
     if half:
@@ -300,13 +321,16 @@
                 span = slice(tile * LANES, (tile + 1) * LANES)
                 row = s * SUBLANES + q * slots
                 summed_ref[:, span] = summed_ref[:, span] + flat_ref[row:row + slots, :]
-    updated = summed_ref[...]
     occupied = lax.broadcasted_iota(jnp.int32, (slots, 1), 0) < count
-    hidden_ref[...] = jnp.where(occupied, updated, 0.0).astype(jnp.bfloat16)
-    normed_out = normalize(updated, next_gain[...])
-    normed_ref[...] = jnp.where(occupied, normed_out, 0.0).astype(jnp.bfloat16)
+    updated_ref[...] = jnp.where(occupied, summed_ref[...], 0.0)
     for copy in outs:
         copy.wait_send()
+
+
+def finish_kernel(updated_ref, next_gain_ref, hidden_ref, normed_ref):
+    updated = updated_ref[...]
+    hidden_ref[...] = updated.astype(jnp.bfloat16)
+    normed_ref[...] = normalize(updated, next_gain_ref[...]).astype(jnp.bfloat16)
 
 
 def fused_layer(n, batch_counts, attn_out, residual_in, norm_gain, w_gate_up, w_down, next_gain):
@@ -319,23 +343,23 @@
     sems = pltpu.SemaphoreType.DMA
     anywhere = pl.BlockSpec(memory_space=pl.ANY)
     in_vmem = pl.BlockSpec(memory_space=pltpu.VMEM)
-    return pl.pallas_call(
+    updated = pl.pallas_call(
         functools.partial(layer_kernel, n, live),
-        out_shape=[jax.ShapeDtypeStruct((slots, width), bf16)] * 2,
-        in_specs=[pl.BlockSpec(memory_space=pltpu.SMEM)] + [anywhere] * 6,
-        out_specs=[in_vmem, in_vmem],
+        out_shape=jax.ShapeDtypeStruct((slots, width), f32),
+        in_specs=[anywhere] * 6,
+        out_specs=in_vmem,
         scratch_shapes=[
+            pltpu.SMEM((1,), jnp.int32),
             pltpu.VMEM((slots, width), bf16),
             pltpu.VMEM((slots, width), bf16),
             pltpu.VMEM((1, width), f32),
-            pltpu.VMEM((1, width), f32),
             pltpu.VMEM(w_gate_up.shape, bf16),
-            pltpu.VMEM((n, hidden_units, depth), bf16),
+            pltpu.VMEM((depth, n * hidden_units), bf16),
             pltpu.VMEM((slots, width), f32),
             pltpu.VMEM((SUBLANES, width // pack + LANES), f32),
             pltpu.VMEM((n, SUBLANES, width // pack + LANES), bf16),
             pltpu.VMEM((live, width), bf16),
-            pltpu.VMEM((n, CHUNKS, live, hidden_units // CHUNKS), bf16),
+            [pltpu.VMEM((n, live, size), bf16) for _, size in chunk_bounds(hidden_units)],
             pltpu.VMEM((live, pack * LANES), f32),
             pltpu.VMEM((n, SUBLANES, LANES), bf16),
             pltpu.VMEM((n, SUBLANES, LANES), bf16),
@@ -359,9 +383,14 @@
         residual_in,
         norm_gain.reshape(1, width),
         w_gate_up,
-        w_down.reshape(n, hidden_units, depth),
-        next_gain.reshape(1, width),
-    )
+        w_down.T,
+    )
+    return pl.pallas_call(
+        finish_kernel,
+        out_shape=[jax.ShapeDtypeStruct((slots, width), bf16)] * 2,
+        in_specs=[in_vmem, in_vmem],
+        out_specs=[in_vmem, in_vmem],
+    )(updated, next_gain.reshape(1, width))
 
 
 def on_device(n, *arrays):
@@ -372,9 +401,11 @@
         n % 4 == 0
         and SUBLANES % slots == 0
         and width % (pack * LANES) == 0
-        and hidden_units % (CHUNKS * LANES) == 0
+        and hidden_units % LANES == 0
+        and hidden_units >= CHUNKS * MXU_DEPTH
         and n * slots // 2 * pack == LANES
         and depth % (LANES // 2) == 0
+        and depth % (4 * SUBLANES) == 0
         and depth + depth % LANES <= pack * LANES
     )
     return tuple(fused_layer(n, *arrays)) if fused else plain_layer(*arrays)

time: 87.8 us -> 53.3 us (0.61)
  local copies, waits for them, and re-layouts: 25 us -> 0 us
  Pallas kernels: 60.8 us -> 51.8 us
    unnamed x3 -> x0, local copies, waits for them, and re-layouts: 25 us -> none
    pallas_call x1 -> x2, Pallas kernels: 60.8 us -> 51.8 us  [the longest x1 50.1 us: fused_layer(): pl.pallas_call(functools.partial(layer_kernel, n, live), out_shape=jax.Sh...]
where the time goes in v2:
time: 53.3 us; the launch traced here: 53.1 us
  Pallas kernels  51.8 us (97%)
  between operations  1.28 us (2%)
    pallas_call x1, Pallas kernels, fused_layer(): pl.pallas_call(functools.partial(layer_kernel, n, live), out_shape=jax.Sh...  50.1 us
    pallas_call x1, Pallas kernels, fused_layer(): pl.pallas_call(finish_kernel, out_shape=[jax.ShapeDtypeStruct((slots, wid...  1.71 us

profile of v2, /device:TPU:0, one launch (start us, length us, event | category | flops | bytes accessed | tf_op | source)
XLA Modules:
  0.0 53.1 jit_solution(4752020148829327484)
XLA Ops:
  1.3 50.1 %shard_map.86.updated_ref = f32[4,7168]{1,0:T(4,128)} custom-call(s32[1]{0:T(128)S(6)} %copy.9.counts_hbm, bf16[4,7168]{1,0:T(4,128)(2,1)} %attn_hbm.1, bf16[4,7168]{1,0:T(4,128)(2,1)} %residual_hbm.1, f32[1,7168]{1,0:T(1,128)} %bitcast.4, bf16[2,1152,7168]{2,1,0:T(8,128)(2,1)} %gate_up_hbm.1, bf16[448,18432]{1,0:T(8,128)(2,1)} %bitcast.3), custom_call_target="tpu_custom_call" | custom-call | tf_op jit(solution)/shard_map/pallas_call | solution.py:346
  51.3 1.7 %shard_map.87 = (bf16[4,7168]{1,0:T(4,128)(2,1)}, bf16[4,7168]{1,0:T(4,128)(2,1)}) custom-call(f32[4,7168]{1,0:T(4,128)} %shard_map.86.updated_ref, f32[1,7168]{1,0:T(1,128)} %bitcast.5), custom_call_target="tpu_custom_call" | custom-call | tf_op jit(solution)/shard_map/pallas_call | solution.py:388

commit v3 on v2

--- a/solution.py
+++ b/solution.py
@@ -44,7 +44,6 @@
 
 LANES = 128
 SUBLANES = 16
-CHUNKS = 3
 MXU_DEPTH = 256
 MESH = pl.DeviceIdType.MESH
 NT = (((1,), (1,)), ((), ()))
@@ -55,10 +54,7 @@
 
 
 def chunk_bounds(units):
-    depths = units // MXU_DEPTH
-    sizes = [MXU_DEPTH * ((depths + CHUNKS - 1 - c) // CHUNKS) for c in range(CHUNKS)]
-    sizes[1] += units - sum(sizes)
-    return [(sum(sizes[:c]), sizes[c]) for c in range(CHUNKS)]
+    return [(at, min(MXU_DEPTH, units - at)) for at in range(0, units, MXU_DEPTH)]
 
 
 class Gather:
@@ -148,6 +144,7 @@
     quarter = width // pack
     units = gate_up.shape[1]
     pieces = chunk_bounds(units)
+    chunks = len(pieces)
     depth = down.shape[0]
 
     barrier = pltpu.get_barrier_semaphore()
@@ -166,7 +163,7 @@
     for copy in small:
         copy.wait()
     weight_copies = []
-    for c in range(CHUNKS):
+    for c in range(chunks):
         for g in range(2):
             span = pl.ds(*pieces[c])
             copy = pltpu.make_async_copy(
@@ -225,51 +222,51 @@
             lambda k, c=c: act_send.at[c, k],
             lambda b, c=c: act_recv.at[c, b],
         )
-        for c in range(CHUNKS)
+        for c in range(chunks)
     ]
 
     def hidden(c):
         first_unit, size = pieces[c]
         span = slice(first_unit, first_unit + size)
         weight_copies[2 * c].wait()
-        gate = lax.dot_general(
-            picked_ref[...], gate_up[0, span, :], NT, preferred_element_type=jnp.float32
-        )
         weight_copies[2 * c + 1].wait()
-        up = lax.dot_general(
-            picked_ref[...], gate_up[1, span, :], NT, preferred_element_type=jnp.float32
-        )
+        both = lax.dot_general(
+            picked_ref[...],
+            gate_up[:, span, :].reshape(2 * size, width),
+            NT,
+            preferred_element_type=jnp.float32,
+        )
+        gate, up = both[:, :size], both[:, size:]
         act_refs[c][me] = (gate / (1.0 + jnp.exp(-gate)) * up).astype(jnp.bfloat16)
         acts[c].start()
 
-    def project(c, total_out):
+    def project(c):
         first_unit, size = pieces[c]
-        for s in range(n):
-            span = slice(s * units + first_unit, s * units + first_unit + size)
-            total_out += lax.dot_general(
-                down[:, span], act_refs[c][s], NT, preferred_element_type=jnp.float32
-            )
-        return total_out
-
-    hidden(0)
-    hidden(1)
-    acts[0].after_far()
-    hidden(2)
-    acts[0].after_near()
-    acts[1].after_far()
-    for copy in down_copies:
-        copy.wait()
-    acts[0].after_core()
-    projected = project(0, jnp.zeros((depth, live), jnp.float32))
-    acts[1].after_near()
-    acts[2].after_far()
-    acts[1].after_core()
-    projected = project(1, projected)
-    acts[2].after_near()
-    acts[2].after_core()
-    projected = project(2, projected)
-
-    wide_ref[:, :depth] = projected.T
+        acts[c].after_core()
+        every = jnp.concatenate([act_refs[c][s] for s in range(n)], axis=1)
+        weights = jnp.concatenate(
+            [down[:, s * units + first_unit:s * units + first_unit + size] for s in range(n)], axis=1
+        )
+        part = lax.dot_general(every, weights, NT, preferred_element_type=jnp.float32)
+        if c == 0:
+            wide_ref[:, :depth] = part
+        else:
+            wide_ref[:, :depth] += part
+
+    far_lag, near_lag, project_lag = 2, 3, 5
+    for step in range(chunks + project_lag):
+        if step < chunks:
+            hidden(step)
+        if step == chunks:
+            for copy in down_copies:
+                copy.wait()
+        if 0 <= step - project_lag < chunks:
+            project(step - project_lag)
+        if 0 <= step - far_lag < chunks:
+            acts[step - far_lag].after_far()
+        if 0 <= step - near_lag < chunks:
+            acts[step - near_lag].after_near()
+
     wide = wide_ref[...]
     half = depth % LANES
     if half:
@@ -339,6 +336,8 @@
     depth = w_down.shape[1]
     live = n * slots // 2
     pack = SUBLANES // slots
+    pieces = chunk_bounds(hidden_units)
+    chunks = len(pieces)
     bf16, f32 = jnp.bfloat16, jnp.float32
     sems = pltpu.SemaphoreType.DMA
     anywhere = pl.BlockSpec(memory_space=pl.ANY)
@@ -359,18 +358,18 @@
             pltpu.VMEM((SUBLANES, width // pack + LANES), f32),
             pltpu.VMEM((n, SUBLANES, width // pack + LANES), bf16),
             pltpu.VMEM((live, width), bf16),
-            [pltpu.VMEM((n, live, size), bf16) for _, size in chunk_bounds(hidden_units)],
+            [pltpu.VMEM((n, live, size), bf16) for _, size in pieces],
             pltpu.VMEM((live, pack * LANES), f32),
             pltpu.VMEM((n, SUBLANES, LANES), bf16),
             pltpu.VMEM((n, SUBLANES, LANES), bf16),
             pltpu.VMEM((n * SUBLANES, LANES), f32),
             sems((4,)),
-            sems((2 * CHUNKS,)),
+            sems((2 * chunks,)),
             sems((4,)),
             sems((n,)),
             sems((n,)),
-            sems((CHUNKS, n)),
-            sems((CHUNKS, n)),
+            sems((chunks, n)),
+            sems((chunks, n)),
             sems((n,)),
             sems((n,)),
         ],
@@ -402,7 +401,7 @@
         and SUBLANES % slots == 0
         and width % (pack * LANES) == 0
         and hidden_units % LANES == 0
-        and hidden_units >= CHUNKS * MXU_DEPTH
+        and hidden_units >= 2 * MXU_DEPTH
         and n * slots // 2 * pack == LANES
         and depth % (LANES // 2) == 0
         and depth % (4 * SUBLANES) == 0

time: 53.3 us -> 50.8 us (0.953)
  Pallas kernels: 51.8 us -> 49.3 us
    pallas_call x1, Pallas kernels: 50.1 us -> 47.6 us  [fused_layer(): pl.pallas_call(functools.partial(layer_kernel, n, live), out_shape=jax.Sh...]
where the time goes in v3:
time: 50.8 us; the launch traced here: 50.6 us
  Pallas kernels  49.3 us (97%)
  between operations  1.28 us (3%)
    pallas_call x1, Pallas kernels, fused_layer(): pl.pallas_call(functools.partial(layer_kernel, n, live), out_shape=jax.Sh...  47.6 us
    pallas_call x1, Pallas kernels, fused_layer(): pl.pallas_call(finish_kernel, out_shape=[jax.ShapeDtypeStruct((slots, wid...  1.71 us

profile of v3, /device:TPU:0, one launch (start us, length us, event | category | flops | bytes accessed | tf_op | source)
XLA Modules:
  0.0 50.6 jit_solution(5538073841316028569)
XLA Ops:
  1.3 47.6 %shard_map.86.updated_ref = f32[4,7168]{1,0:T(4,128)} custom-call(s32[1]{0:T(128)S(6)} %copy.9.counts_hbm, bf16[4,7168]{1,0:T(4,128)(2,1)} %attn_hbm.1, bf16[4,7168]{1,0:T(4,128)(2,1)} %residual_hbm.1, f32[1,7168]{1,0:T(1,128)} %bitcast.4, bf16[2,1152,7168]{2,1,0:T(8,128)(2,1)} %gate_up_hbm.1, bf16[448,18432]{1,0:T(8,128)(2,1)} %bitcast.3), custom_call_target="tpu_custom_call" | custom-call | tf_op jit(solution)/shard_map/pallas_call | solution.py:345
  48.9 1.7 %shard_map.87 = (bf16[4,7168]{1,0:T(4,128)(2,1)}, bf16[4,7168]{1,0:T(4,128)(2,1)}) custom-call(f32[4,7168]{1,0:T(4,128)} %shard_map.86.updated_ref, f32[1,7168]{1,0:T(1,128)} %bitcast.5), custom_call_target="tpu_custom_call" | custom-call | tf_op jit(solution)/shard_map/pallas_call | solution.py:387

commit v4 on v3

--- a/solution.py
+++ b/solution.py
@@ -102,7 +102,7 @@
             yield far
 
     def start(self):
-        for far in reversed(self.lines):
+        for far in self.lines:
             self.send(self.me, self.index(far, self.near, self.core))
         self.send(self.me, self.across)
         self.send(self.me, self.sibling)

time: 50.8 us -> 50.2 us (0.988)
  Pallas kernels: 49.3 us -> 48.7 us
    pallas_call x1, Pallas kernels: 47.6 us -> 47 us  [fused_layer(): pl.pallas_call(functools.partial(layer_kernel, n, live), out_shape=jax.Sh...]
where the time goes in v4:
time: 50.2 us; the launch traced here: 50 us
  Pallas kernels  48.7 us (97%)
  between operations  1.28 us (3%)
    pallas_call x1, Pallas kernels, fused_layer(): pl.pallas_call(functools.partial(layer_kernel, n, live), out_shape=jax.Sh...  47 us
    pallas_call x1, Pallas kernels, fused_layer(): pl.pallas_call(finish_kernel, out_shape=[jax.ShapeDtypeStruct((slots, wid...  1.71 us

profile of v4, /device:TPU:0, one launch (start us, length us, event | category | flops | bytes accessed | tf_op | source)
XLA Modules:
  0.0 50.0 jit_solution(2540614322630331837)
XLA Ops:
  1.3 47.0 %shard_map.86.updated_ref = f32[4,7168]{1,0:T(4,128)} custom-call(s32[1]{0:T(128)S(6)} %copy.9.counts_hbm, bf16[4,7168]{1,0:T(4,128)(2,1)} %attn_hbm.1, bf16[4,7168]{1,0:T(4,128)(2,1)} %residual_hbm.1, f32[1,7168]{1,0:T(1,128)} %bitcast.4, bf16[2,1152,7168]{2,1,0:T(8,128)(2,1)} %gate_up_hbm.1, bf16[448,18432]{1,0:T(8,128)(2,1)} %bitcast.3), custom_call_target="tpu_custom_call" | custom-call | tf_op jit(solution)/shard_map/pallas_call | solution.py:345
  48.3 1.7 %shard_map.87 = (bf16[4,7168]{1,0:T(4,128)(2,1)}, bf16[4,7168]{1,0:T(4,128)(2,1)}) custom-call(f32[4,7168]{1,0:T(4,128)} %shard_map.86.updated_ref, f32[1,7168]{1,0:T(1,128)} %bitcast.5), custom_call_target="tpu_custom_call" | custom-call | tf_op jit(solution)/shard_map/pallas_call | solution.py:387
